TPU v7x, 128 devices: a whole 4x4x4 slice. The times are simulated.
128 devices in a mesh: gx: 8 (over x, core), gy: 16 (over z, y).
Axes of the slice: x: 4, y: 4, z: 4, core: 2. Of those that a mesh axis runs over, the one named last changes fastest.
Arguments:
- state: float32 [1024, 1024, 128], P('gx', 'gy'), may hold values from -6 to 6
- diffusion: float32 [1024, 1024, 128], P('gx', 'gy'), may hold values from 0.01 to 0.12
- vert_inverse: float32 [1024, 128, 128], P('gy'), as said below
- profiles: bfloat16 [131072, 128], P(('gx', 'gy')), may hold values from -6 to 6
- counts: int32 [128, 128], P(('gx', 'gy')), may hold values from 0 to 16, as said below
- cell_lon: int32 [131072], P(('gx', 'gy')), may hold values from 0 to 127
- cell_lat: int32 [131072], P(('gx', 'gy')), may hold values from 0 to 63
- weight_slot: int32 [2, 131072], P(None, ('gx', 'gy')), may hold values from 0 to 63
Outputs:
- adjoint: float32 [1024, 1024, 128], P('gx', 'gy')
Inputs may be any that keep to these rules, and one draw needn't show every extreme that they name: Each row s sums to 1024; source device s stores its profiles in order of subdomain, counts[s,d] of them for subdomain d, which covers longitude cells (d // 16) * 128 onwards and latitude cells (d % 16) * 64 onwards. Some subdomain receives 16 profiles from every source. `vert_inverse`: one matrix for each latitude row.
All inputs are finite; a program needn't handle non-finite values.
Results may differ from a plain program's by a relative error of at most 0.0015.
Values may be sent and summed in bfloat16 or wider, within the bound.
A program may use at most 128 MiB of HBM per device.

v0:
```python
import functools

import jax
import jax.numpy as jnp
from jax import lax
from jax.experimental import pallas as pl
from jax.experimental.pallas import tpu as pltpu
from jax.sharding import PartitionSpec as P

CAP = 16
MESH = pl.DeviceIdType.MESH

ACCS = 4
EDGE = 8
CLEAR = 64


def split(value):
    high = value.astype(jnp.bfloat16)
    low = (value - high.astype(jnp.float32)).astype(jnp.bfloat16)
    return jnp.concatenate([high, low], axis=1)


def exchange_body(n_gx, n_gy, unused_lat, counts_ref, prof_ref, lon_ref, lat_ref, weight_ref, state_ref, diff_ref,
                  inv_ref, prof_out, meta_out, diff_out, inv_out, inv_halo, diff_rows, diff_cols, acc0, acc1, acc2, acc3,
                  counts, prof, lon, lat, weight, wide, table, prof_send, meta_send, inv_stage, state_stage, diff_stage, row_stage, high_stage,
                  load_sem, psend, precv, msend, mrecv, hsend, hrecv):
    held, levels = prof_ref.shape
    peers = prof_out.shape[0]
    nx, ny, _ = state_ref.shape
    pitch = state_stage.shape[0] // nx
    wide_x = nx + EDGE
    gx = lax.axis_index("gx")
    gy = lax.axis_index("gy")
    me = gx * n_gy + gy
    small = [
        pltpu.make_async_copy(src, dst, load_sem.at[k])
        for k, (src, dst) in enumerate(
            [(counts_ref, counts), (prof_ref, prof), (lon_ref, lon), (lat_ref, lat), (weight_ref, weight)])
    ]
    large = [
        pltpu.make_async_copy(diff_ref, diff_stage.reshape(nx, pitch, levels).at[:, 0:ny, :], load_sem.at[5]),
        pltpu.make_async_copy(inv_ref, inv_stage, load_sem.at[6]),
        pltpu.make_async_copy(state_ref, state_stage.reshape(nx, pitch, levels).at[:, 0:ny, :], load_sem.at[7]),
    ]
    for copy in small + large:
        copy.start()

    def peer(i):
        y = lax.rem(lax.rem(gy, 4) + lax.rem(i, 4) + 2, 4)
        z = lax.rem(lax.div(gy, 4) + lax.rem(lax.div(i, 4), 4) + n_gy // 8, n_gy // 4)
        x = lax.rem(lax.div(gx, 2) + lax.rem(lax.div(i, n_gy), n_gx // 2) + n_gx // 4, n_gx // 2)
        c = lax.rem(gx + lax.div(i, n_gy * (n_gx // 2)), 2)
        return x * 2 + c, z * 4 + y

    own = 2 + (n_gy // 8) * 4 + (n_gx // 4) * n_gy

    def each_peer(do):
        for first, last in ((0, own), (own + 1, peers)):

            @pl.loop(first, last)
            def _(i):
                do(*peer(i))

    barrier = pltpu.get_barrier_semaphore()
    each_peer(lambda x, y: pl.semaphore_signal(barrier, inc=1, device_id=(x, y), device_id_type=MESH))

    for copy in small:
        copy.wait()
    blocks = held // 128
    wide[0:held, :] = prof[...].astype(jnp.float32)
    wide[held:held + CAP, :] = jnp.zeros((CAP, levels), jnp.float32)
    for b in range(blocks):
        table[b, 0:1, :] = lon[b:b + 1, :]
        table[b, 1:2, :] = lat[b:b + 1, :]
        table[b, 2:4, :] = weight[:, b * 128:(b + 1) * 128]
        table[b, 4:8, :] = jnp.zeros((4, 128), jnp.int32)
    for b in range(blocks, blocks + 2):
        table[b] = jnp.zeros((8, 128), jnp.int32)
    lane = lax.broadcasted_iota(jnp.int32, (8, 128), 1)
    field = lax.broadcasted_iota(jnp.int32, (8, 128), 0)

    def one(d, start):
        count = counts[0, d]
        prof_send[d] = wide[pl.ds(start, CAP), :].astype(jnp.bfloat16)
        at = lax.rem(start, 128)
        b = lax.div(start, 128)
        back = lax.rem(128 - at, 128)
        here = pltpu.roll(table[b], back, 1)
        there = pltpu.roll(table[b + 1], back, 1)
        got = jnp.where(lane < 128 - at, here, there)
        got = jnp.where((field == 1) & (lane >= count), unused_lat, got)
        row = jnp.where((field == 0) & (lane < CAP), got, 0)
        for f in range(1, 4):
            moved = pltpu.roll(got, f * CAP, 1)
            row = row + jnp.where((field == f) & (lane >= f * CAP) & (lane < (f + 1) * CAP), moved, 0)
        meta_send[pl.ds(d, 1), :] = jnp.sum(row, axis=0, keepdims=True)
        return start + count

    lax.fori_loop(0, peers, one, jnp.int32(0), unroll=16)

    def remote(src, dst, ssem, rsem, x, y):
        return pltpu.make_async_remote_copy(
            src_ref=src, dst_ref=dst, send_sem=ssem, recv_sem=rsem, device_id=(x, y), device_id_type=MESH)

    has_n = gy < n_gy - 1
    has_s = gy > 0
    up = jnp.minimum(gy + 1, n_gy - 1)
    down = jnp.maximum(gy - 1, 0)
    e = lax.rem(gx + 1, n_gx)
    w = lax.rem(gx + n_gx - 1, n_gx)

    def halo(k, src, dst, x, y):
        return remote(src, dst, hsend.at[k], hrecv.at[k], x, y)

    to_e = halo(0, diff_stage.at[(nx - 1) * pitch:(nx - 1) * pitch + ny], diff_cols.at[0], e, gy)
    to_w = halo(1, diff_stage.at[0:ny], diff_cols.at[1], w, gy)
    to_n = [halo(2, row_stage.at[1], diff_rows.at[1], gx, up),
            halo(3, high_stage.at[1], inv_halo.at[1], gx, up)]
    to_s = [halo(4, row_stage.at[0], diff_rows.at[0], gx, down),
            halo(5, high_stage.at[0], inv_halo.at[0], gx, down)]
    large[0].wait()
    large[1].wait()
    for k, y in ((0, 0), (1, ny - 1)):
        row_stage[k] = diff_stage[pl.ds(y, nx, stride=pitch), :].astype(jnp.bfloat16)
        high_stage[k] = inv_stage[y].astype(jnp.bfloat16)
    pl.semaphore_wait(barrier, peers - 1)

    def send(x, y):
        to = x * n_gy + y
        remote(prof_send.at[to], prof_out.at[me], psend, precv, x, y).start()
        remote(meta_send.at[pl.ds(to, 1)], meta_out.at[pl.ds(me, 1)], msend, mrecv, x, y).start()

    each_peer(send)
    to_e.start()
    to_w.start()

    @pl.when(has_n)
    def _():
        for copy in to_n:
            copy.start()

    @pl.when(has_s)
    def _():
        for copy in to_s:
            copy.start()

    prof_out[me] = prof_send[me]
    meta_out[pl.ds(me, 1), :] = meta_send[pl.ds(me, 1), :]
    empty = jnp.zeros((CLEAR, levels), jnp.float32)

    @pl.loop(0, acc1.shape[0] // CLEAR)
    def _(i):
        rows = pl.ds(pl.multiple_of(i * CLEAR, CLEAR), CLEAR)
        for acc in (acc1, acc2, acc3):
            acc[rows, :] = empty

    @pl.loop(0, ny, unroll=4)
    def _(y):
        inv_out[y] = split(inv_stage[y])

    large[2].wait()
    margin = jnp.zeros((EDGE, levels), jnp.float32)

    @pl.loop(0, ny, unroll=2)
    def _(y):
        first = pl.multiple_of(y * wide_x, 8)
        acc0[pl.ds(first, nx), :] = state_stage[pl.ds(y, nx, stride=pitch), :]
        acc0[pl.ds(first + nx, EDGE), :] = margin
        diff_out[y] = diff_stage[pl.ds(y, nx, stride=pitch), :]

    tail = acc0.shape[0] - ny * wide_x
    acc0[ny * wide_x:, :] = jnp.zeros((tail, levels), jnp.float32)
    n = peers - 1
    whole_p = remote(prof_send.at[0:n], prof_out.at[0:n], psend, precv, gx, gy)
    whole_m = remote(meta_send.at[0:n], meta_out.at[0:n], msend, mrecv, gx, gy)
    whole_p.wait_recv()
    whole_m.wait_recv()
    whole_p.wait_send()
    whole_m.wait_send()
    for copy in (to_e, to_w):
        copy.wait_send()
        copy.wait_recv()

    @pl.when(has_n)
    def _():
        for copy in to_n:
            copy.wait_send()
        for copy in to_s:
            copy.wait_recv()

    @pl.when(has_s)
    def _():
        for copy in to_s:
            copy.wait_send()
        for copy in to_n:
            copy.wait_recv()


def exchange(counts, prof, lon, lat, weight, state, diff, inv, unused_lat, n_gx, n_gy):
    held, levels = prof.shape
    nx, ny, _ = state.shape
    peers = counts.shape[1]
    vm = pltpu.VMEM
    dma = pltpu.SemaphoreType.DMA
    hbm = functools.partial(pltpu.with_memory_space_constraint, memory_space=pltpu.HBM)
    args = (counts, prof, lon.reshape(-1, 128), lat.reshape(-1, 128), weight, state, diff, inv)
    pitched = (nx * (ny + 8), levels)
    rows = -(-(ny + 3) * (nx + EDGE) // CLEAR) * CLEAR
    return pl.pallas_call(
        functools.partial(exchange_body, n_gx, n_gy, unused_lat),
        out_shape=(
            vm((peers, CAP, levels), jnp.bfloat16),
            vm((peers, 128), jnp.int32),
            vm((ny, nx, levels), jnp.float32),
            vm((ny, levels, 2 * levels), jnp.bfloat16),
            vm((2, levels, levels), jnp.bfloat16),
            vm((2, nx, levels), jnp.bfloat16),
            vm((2, ny, levels), jnp.float32),
            *[vm((rows, levels), jnp.float32)] * ACCS,
        ),
        in_specs=[pl.BlockSpec(memory_space=pltpu.HBM)] * 8,
        out_specs=[pl.BlockSpec(memory_space=vm)] * (7 + ACCS),
        scratch_shapes=[
            pltpu.SMEM((1, peers), jnp.int32),
            vm((held, levels), jnp.bfloat16),
            vm((held // 128, 128), jnp.int32),
            vm((held // 128, 128), jnp.int32),
            vm((2, held), jnp.int32),
            vm((held + CAP, levels), jnp.float32),
            vm((held // 128 + 2, 8, 128), jnp.int32),
            vm((peers, CAP, levels), jnp.bfloat16),
            vm((peers, 128), jnp.int32),
            vm((ny, levels, levels), jnp.float32),
            vm(pitched, jnp.float32),
            vm(pitched, jnp.float32),
            vm((2, nx, levels), jnp.bfloat16),
            vm((2, levels, levels), jnp.bfloat16),
            dma((8,)), dma, dma, dma, dma, dma((6,)), dma((6,)),
        ],
        compiler_params=pltpu.CompilerParams(
            collective_id=0, has_side_effects=True, vmem_limit_bytes=17 * 1024 * 1024),
        name="exchange",
    )(*[hbm(a) for a in args])


SLOTS = 64


def scatter_body(nx, ny, prof_ref, meta_ref, *rest):
    peers, cap, levels = prof_ref.shape
    pitch = nx + EDGE
    accs = rest[ACCS:2 * ACCS]
    edge_e, edge_w, edge_n, edge_s, knot, table, index_v, index_s, index_sem = rest[2 * ACCS:]
    meta = meta_ref[...]
    lat_up = pltpu.roll(meta, 128 - cap, 1)
    index_v[...] = lat_up * pitch + meta
    index_copy = pltpu.make_async_copy(index_v, index_s, index_sem)
    index_copy.start()
    group = 8
    lane = lax.broadcasted_iota(jnp.int32, (group, cap, 128), 2)
    slot = lax.broadcasted_iota(jnp.int32, (group, cap, 128), 1)
    own = (lane % cap == slot).astype(jnp.float32)
    r = lax.broadcasted_iota(jnp.int32, (128, 2 * levels), 0) // cap
    c = lax.broadcasted_iota(jnp.int32, (128, 2 * levels), 1) // levels
    pick = (r == c + 2).astype(jnp.bfloat16)

    @pl.loop(0, peers // group, unroll=4)
    def _(i):
        m = meta_ref[pl.ds(pl.multiple_of(i * group, group), group), :].astype(jnp.float32)
        spread = (m[:, None, :] * own).reshape(group * cap, 128).astype(jnp.bfloat16)
        frac = jnp.dot(spread, pick, preferred_element_type=jnp.float32) * (1.0 / SLOTS)
        fx = frac[:, :levels]
        fy = frac[:, levels:]
        p = prof_ref[pl.ds(i * group, group)].reshape(group * cap, levels).astype(jnp.float32)
        p1 = p * fx
        p0 = p - p1
        q01 = p0 * fy
        q11 = p1 * fy
        base = i * (group * cap * 4)
        n = group * cap
        table[pl.ds(base, n, stride=4), :] = p0 - q01
        table[pl.ds(base + 1, n, stride=4), :] = p1 - q11
        table[pl.ds(base + 2, n, stride=4), :] = q01
        table[pl.ds(base + 3, n, stride=4), :] = q11

    index_copy.wait()

    @pl.loop(0, peers)
    def _(s):
        first = pl.multiple_of(s * (cap * 4), cap * 4)
        for k in range(0, cap, ACCS):
            for j in range(ACCS):
                at = index_s[s, k + j]
                row = first + (k + j) * 4
                acc = accs[j]
                acc[pl.ds(at, 2), :] += table[pl.ds(row, 2), :]
                acc[pl.ds(at + pitch, 2), :] += table[pl.ds(row + 2, 2), :]

    def total(at, n):
        out = accs[0][pl.ds(at, n), :]
        for acc in accs[1:]:
            out = out + acc[pl.ds(at, n), :]
        return out

    @pl.loop(0, ny, unroll=8)
    def _(y):
        first = pl.multiple_of(y * pitch, 8)
        edge_w[pl.ds(y, 1), :] = total(first, 8)[0:1]
        edge_e[pl.ds(y, 1), :] = total(first + nx - 8, 8)[7:8]
        edge_e[pl.ds(ny + y, 1), :] = total(first + nx, 8)[0:1]

    edge_s[...] = total(0, nx).astype(edge_s.dtype)
    edge_n[0] = total((ny - 1) * pitch, nx).astype(edge_n.dtype)
    edge_n[1] = total(ny * pitch, nx).astype(edge_n.dtype)
    corner = total(ny * pitch + nx, 8)
    edge_e[2 * ny:2 * ny + 8, :] = corner
    knot[0:1, :] = corner[0:1]
    knot[1:2, :] = total((ny - 1) * pitch + nx, 8)[0:1]
    knot[2:3, :] = total(ny * pitch + nx - 8, 8)[7:8]
    knot[3:4, :] = total(nx, 8)[0:1]
    knot[4:5, :] = total(ny * pitch, 8)[0:1]
    knot[5:8, :] = jnp.zeros((3, levels), jnp.float32)


def scatter(prof, meta, accs, nx, ny):
    peers, cap, levels = prof.shape
    vm = pltpu.VMEM
    block = pl.BlockSpec(memory_space=vm)
    return pl.pallas_call(
        functools.partial(scatter_body, nx, ny),
        out_shape=(
            *[vm(accs[0].shape, jnp.float32)] * ACCS,
            vm((2 * ny + 8, levels), jnp.float32),
            vm((ny, levels), jnp.float32),
            vm((2, nx, levels), jnp.bfloat16),
            vm((nx, levels), jnp.bfloat16),
            vm((8, levels), jnp.float32),
        ),
        in_specs=[block] * (2 + ACCS),
        out_specs=[block] * (5 + ACCS),
        scratch_shapes=[
            vm((peers * cap * 4 + 8, levels), jnp.float32),
            vm((peers, 128), jnp.int32),
            pltpu.SMEM((peers, 128), jnp.int32),
            pltpu.SemaphoreType.DMA,
        ],
        input_output_aliases={2 + k: k for k in range(ACCS)},
        compiler_params=pltpu.CompilerParams(vmem_limit_bytes=5 * 1024 * 1024),
        name="scatter",
    )(prof, meta, *accs)


STEPS = 4
CHUNK = 16


def steps_body(n_gx, n_gy, acc0, acc1, acc2, acc3, edge_e, edge_w, edge_n, edge_s, knot,
               diff_ref, inv_pair, inv_halo, diff_rows, diff_cols, out_ref,
               mu_ref, g_last, g_other, col_send, col_recv, row_send, row_recv, in_w, in_e, in_s, in_n, knots,
               spill_send, spill_recv, col_ssem, col_rsem, row_ssem, row_rsem):
    ny, nx, levels = diff_ref.shape
    pitch = nx + EDGE
    gx = lax.axis_index("gx")
    gy = lax.axis_index("gy")
    e = lax.rem(gx + 1, n_gx)
    w = lax.rem(gx + n_gx - 1, n_gx)
    has_n = gy < n_gy - 1
    has_s = gy > 0
    up = jnp.minimum(gy + 1, n_gy - 1)
    down = jnp.maximum(gy - 1, 0)
    barrier = pltpu.get_barrier_semaphore()

    def greet(x, y):
        pl.semaphore_signal(barrier, inc=1, device_id=(x, y), device_id_type=MESH)

    greet(e, gy)
    greet(w, gy)

    @pl.when(has_n)
    def _():
        greet(gx, up)
        greet(e, up)
        greet(w, up)

    @pl.when(has_s)
    def _():
        greet(gx, down)
        greet(e, down)
        greet(w, down)

    pl.semaphore_wait(barrier, 2 + 3 * has_n.astype(jnp.int32) + 3 * has_s.astype(jnp.int32))

    def remote(src, dst, ssem, rsem, x, y):
        return pltpu.make_async_remote_copy(
            src_ref=src, dst_ref=dst, send_sem=ssem, recv_sem=rsem, device_id=(x, y), device_id_type=MESH)

    def spill(k, src, dst, x, y):
        return remote(src, dst, spill_send.at[k], spill_recv.at[k], x, y)

    across = [spill(0, edge_e, in_w, e, gy), spill(1, edge_w, in_e, w, gy)]
    north_to = [spill(2, edge_n, in_s, gx, up), spill(4, knot, knots.at[0], e, up),
                spill(6, knot, knots.at[2], w, up), spill(7, knot, knots.at[3], gx, up)]
    south_to = [spill(3, edge_s, in_n, gx, down), spill(5, knot, knots.at[1], e, down)]
    for copy in across:
        copy.start()

    @pl.when(has_n)
    def _():
        for copy in north_to:
            copy.start()

    @pl.when(has_s)
    def _():
        for copy in south_to:
            copy.start()

    zeros = jnp.zeros((nx + 2 * EDGE, levels), jnp.float32)

    @pl.when(jnp.logical_not(has_s))
    def _():
        g_other[0] = zeros
        g_last[0] = zeros

    @pl.when(jnp.logical_not(has_n))
    def _():
        g_other[ny + 1] = zeros
        g_last[ny + 1] = zeros

    chunks = ny // CHUNK

    def cols(n, side, c):
        rows = pl.ds(pl.multiple_of(c * CHUNK, CHUNK), CHUNK)
        return remote(col_send.at[n, side, rows], col_recv.at[n, side, rows],
                      col_ssem.at[n, side, c], col_rsem.at[n, side, c], e if side == 0 else w, gy)

    def flux(n):
        return g_last if (STEPS - 1 - n) % 2 == 0 else g_other

    def rowcopy(n, side):
        return remote(row_send.at[n, side], row_recv.at[n, side],
                      row_ssem.at[n, side], row_rsem.at[n, side], gx, up if side == 0 else down)

    def stencil(g, y):
        mid = g[y + 1, pl.ds(EDGE, nx), :]
        near = (g[y + 1, pl.ds(EDGE - 1, nx), :] + g[y + 1, pl.ds(EDGE + 1, nx), :]) + (
            g[y, pl.ds(EDGE, nx), :] + g[y + 2, pl.ds(EDGE, nx), :])
        return mu_ref[y] + (near - 4.0 * mid)

    first_lane = lax.broadcasted_iota(jnp.int32, (8, levels), 0) == 0

    side_lane = lax.broadcasted_iota(jnp.int32, (16, levels), 0)

    def sides(y):
        spilled = in_w[pl.ds(ny + y, 1), :]
        west = in_w[pl.ds(y, 1), :]
        east = in_e[pl.ds(y, 1), :] + edge_e[pl.ds(ny + y, 1), :]
        lam = jnp.where(side_lane == 0, spilled, jnp.where(side_lane == 1, west, jnp.where(side_lane == 2, east, 0.0)))
        mu = jnp.dot(lam.astype(jnp.bfloat16), inv_pair[y, :, 0:levels], preferred_element_type=jnp.float32)
        g = flux(0)
        mu_ref[y, 0:1, :] += mu[0:1]
        g[y + 1, EDGE:EDGE + 1, :] += diff_ref[y, 0:1, :] * mu[0:1]
        g[y + 1, EDGE - 1:EDGE, :] = diff_cols[0, pl.ds(y, 1), :] * mu[1:2]
        g[y + 1, EDGE + nx:EDGE + nx + 1, :] = diff_cols[1, pl.ds(y, 1), :] * mu[2:3]

    def beside(lam, extra):
        head = lam[0:8] + jnp.where(first_lane, extra, 0.0)
        return jnp.concatenate([head, lam[8:]], axis=0).astype(jnp.bfloat16)

    def mixed(lam, y):
        pair = inv_pair[y]
        both = jnp.dot(split(lam), jnp.concatenate([pair, pair], axis=0), preferred_element_type=jnp.float32)
        mu = both[:, :levels] + both[:, levels:]
        return mu, diff_ref[y] * mu

    def neighbours_in():
        @pl.when(has_s)
        def _():
            for copy in north_to:
                copy.wait_recv()
            fresh, g = mixed(in_s[1].astype(jnp.float32), 0)
            mu_ref[0] += fresh
            flux(0)[1, EDGE:EDGE + nx, :] += g
            in_w[ny:ny + 1, :] += knots[0, 0:1, :]
            in_w[0:1, :] += knots[0, 2:3, :]
            in_e[0:1, :] += knots[2, 4:5, :] + knots[3, 0:1, :]
            lam = beside(in_s[0].astype(jnp.float32), knots[0, 1:2, :])
            mu = jnp.dot(lam, inv_halo[1], preferred_element_type=jnp.float32)
            flux(0)[0, EDGE:EDGE + nx, :] = diff_rows[1].astype(jnp.float32) * mu

        @pl.when(has_n)
        def _():
            for copy in south_to:
                copy.wait_recv()
            lam = beside(in_n[...].astype(jnp.float32) + edge_n[1].astype(jnp.float32),
                         knots[1, 3:4, :] + in_w[2 * ny:2 * ny + 1, :])
            mu = jnp.dot(lam, inv_halo[0], preferred_element_type=jnp.float32)
            flux(0)[ny + 1, EDGE:EDGE + nx, :] = diff_rows[0].astype(jnp.float32) * mu

    def row(n, y):
        if n > 0:
            return mixed(stencil(flux(n - 1), y), y)
        rows = pl.ds(pl.multiple_of(y * pitch, 8), nx)
        return mixed((acc0[rows, :] + acc1[rows, :]) + (acc2[rows, :] + acc3[rows, :]), y)

    def columns_in(n, c):
        for side in range(2):
            cols(n, side, c).wait_recv()
        for r in range(CHUNK):
            y = c * CHUNK + r
            flux(n)[y + 1, EDGE - 1:EDGE, :] = col_recv[n, 0, pl.ds(y, 1), :]
            flux(n)[y + 1, EDGE + nx:EDGE + nx + 1, :] = col_recv[n, 1, pl.ds(y, 1), :]

    def rows_in(n):
        @pl.when(has_s)
        def _():
            rowcopy(n, 0).wait_recv()
            flux(n)[0, EDGE:EDGE + nx, :] = row_recv[n, 0].astype(jnp.float32)

        @pl.when(has_n)
        def _():
            rowcopy(n, 1).wait_recv()
            flux(n)[ny + 1, EDGE:EDGE + nx, :] = row_recv[n, 1].astype(jnp.float32)

    def north_out(n):
        @pl.when(has_n)
        def _():
            rowcopy(n, 0).start()

    def south_out(n):
        @pl.when(has_s)
        def _():
            rowcopy(n, 1).start()

    for n in range(STEPS):
        if n > 0:
            if n > 1:
                columns_in(n - 1, chunks - 1)
                columns_in(n - 1, 0)
                rows_in(n - 1)
            row_send[n, 0] = row(n, ny - 1)[1].astype(row_send.dtype)
            row_send[n, 1] = row(n, 0)[1].astype(row_send.dtype)
            north_out(n)
            south_out(n)

        @pl.loop(0, chunks)
        def _(i):
            c = lax.rem(i + chunks - 1, chunks)
            if n > 1:

                @pl.when(i > 1)
                def _():
                    columns_in(n - 1, c)

            for r in range(CHUNK):
                y = c * CHUNK + r
                mu, g = row(n, y)
                mu_ref[y] = mu
                flux(n)[y + 1, pl.ds(EDGE, nx), :] = g
                if n > 0:
                    col_send[n, 0, pl.ds(y, 1), :] = g[nx - 1:nx]
                    col_send[n, 1, pl.ds(y, 1), :] = g[0:1]

            if n > 0:
                for side in range(2):
                    cols(n, side, c).start()

        if n == 0:
            for copy in across:
                copy.wait_recv()

            @pl.loop(0, chunks)
            def _(i):
                c = chunks - 1 - i
                pl.when(i == chunks - 1)(neighbours_in)
                for r in range(CHUNK):
                    sides(c * CHUNK + r)

    last = STEPS - 1

    out_pitch = out_ref.shape[0] // nx
    nothing = jnp.zeros((1, levels), jnp.float32)
    g_last[0] = zeros
    g_last[ny + 1] = zeros

    @pl.loop(0, chunks)
    def _(c):
        for r in range(CHUNK):
            y = c * CHUNK + r
            g_last[y + 1, EDGE - 1:EDGE, :] = nothing
            g_last[y + 1, EDGE + nx:EDGE + nx + 1, :] = nothing

    @pl.loop(0, chunks)
    def _(c):
        for r in range(CHUNK):
            y = c * CHUNK + r
            out_ref[pl.ds(y, nx, stride=out_pitch), :] = stencil(g_last, y)

    @pl.loop(0, chunks)
    def _(c):
        for side in range(2):
            cols(last, side, c).wait_recv()

    east_edge = (nx - 1) * out_pitch
    out_ref[0:ny, :] += col_recv[last, 0]
    out_ref[east_edge:east_edge + ny, :] += col_recv[last, 1]

    @pl.when(has_s)
    def _():
        rowcopy(last, 0).wait_recv()
        out_ref[pl.ds(0, nx, stride=out_pitch), :] += row_recv[last, 0].astype(jnp.float32)

    @pl.when(has_n)
    def _():
        rowcopy(last, 1).wait_recv()
        out_ref[pl.ds(ny - 1, nx, stride=out_pitch), :] += row_recv[last, 1].astype(jnp.float32)

    @pl.when(has_s)
    def _():
        for n in range(1, STEPS):
            rowcopy(n, 1).wait_send()
        for copy in south_to:
            copy.wait_send()

    @pl.when(has_n)
    def _():
        for n in range(1, STEPS):
            rowcopy(n, 0).wait_send()
        for copy in north_to:
            copy.wait_send()

    for copy in across:
        copy.wait_send()
    for n in range(1, STEPS):

        @pl.loop(0, chunks)
        def _(c):
            for side in range(2):
                cols(n, side, c).wait_send()


def steps(accs, edges, diffusion, inverse, halos, n_gx, n_gy, space=None):
    ny, nx, levels = diffusion.shape
    vm = pltpu.VMEM
    chunks = ny // CHUNK
    dma = pltpu.SemaphoreType.DMA
    make = space or (lambda s, d: jax.ShapeDtypeStruct(s, d))
    return pl.pallas_call(
        functools.partial(steps_body, n_gx, n_gy),
        out_shape=make((nx * (ny + 8), levels), jnp.float32),
        in_specs=[pl.BlockSpec(memory_space=vm)] * (10 + ACCS),
        out_specs=pl.BlockSpec(memory_space=vm),
        scratch_shapes=[
            vm((ny, nx, levels), jnp.float32),
            vm((ny + 2, nx + 2 * EDGE, levels), jnp.float32),
            vm((ny + 2, nx + 2 * EDGE, levels), jnp.float32),
            vm((STEPS, 2, ny, levels), jnp.float32),
            vm((STEPS, 2, ny, levels), jnp.float32),
            vm((STEPS, 2, nx, levels), jnp.bfloat16),
            vm((STEPS, 2, nx, levels), jnp.bfloat16),
            vm((2 * ny + 8, levels), jnp.float32),
            vm((ny, levels), jnp.float32),
            vm((2, nx, levels), jnp.bfloat16),
            vm((nx, levels), jnp.bfloat16),
            vm((4, 8, levels), jnp.float32),
            dma((8,)), dma((8,)),
            dma((STEPS, 2, chunks)), dma((STEPS, 2, chunks)), dma((STEPS, 2)), dma((STEPS, 2)),
        ],
        compiler_params=pltpu.CompilerParams(
            collective_id=1, has_side_effects=True, vmem_limit_bytes=17 * 1024 * 1024),
        name="steps",
    )(*accs, *edges, diffusion, inverse, *halos)


def finish_body(parts, stage, out_ref, sems):
    nx, ny, levels = out_ref.shape
    wide = stage.reshape(nx, stage.shape[0] // nx, levels)
    step = nx // parts
    copies = [
        pltpu.make_async_copy(wide.at[k * step:(k + 1) * step, 0:ny, :], out_ref.at[k * step:(k + 1) * step], sems.at[k])
        for k in range(parts)
    ]
    for copy in copies:
        copy.start()
    for copy in copies:
        copy.wait()


def finish(stage, nx, ny):
    levels = stage.shape[1]
    parts = 8
    return pl.pallas_call(
        functools.partial(finish_body, parts),
        out_shape=jax.ShapeDtypeStruct((nx, ny, levels), jnp.float32),
        in_specs=[pl.BlockSpec(memory_space=pltpu.VMEM)],
        out_specs=pl.BlockSpec(memory_space=pltpu.HBM),
        scratch_shapes=[pltpu.SemaphoreType.DMA((parts,))],
        compiler_params=pltpu.CompilerParams(vmem_limit_bytes=1024 * 1024),
        name="finish",
    )(stage)


def shards(n_gx, n_gy, state, diffusion, vert_inverse, profiles, counts, cell_lon, cell_lat, weight_slot):
    nx, ny, _ = state.shape
    got, got_meta, diffusion, inverse, *rest = exchange(
        counts, profiles, cell_lon, cell_lat, weight_slot, state, diffusion, vert_inverse, ny + 1, n_gx, n_gy)
    made = scatter(got, got_meta, rest[3:], nx, ny)
    stage = steps(made[:ACCS], made[ACCS:], diffusion, inverse, rest[:3], n_gx, n_gy, pltpu.VMEM)
    return finish(stage, nx, ny)


def solution(mesh):
    return jax.shard_map(
        functools.partial(shards, mesh.shape["gx"], mesh.shape["gy"]),
        mesh=mesh,
        in_specs=(
            P("gx", "gy", None),
            P("gx", "gy", None),
            P("gy", None, None),
            P(("gx", "gy"), None),
            P(("gx", "gy"), None),
            P(("gx", "gy")),
            P(("gx", "gy")),
            P(None, ("gx", "gy")),
        ),
        out_specs=P("gx", "gy", None),
        check_vma=False,
    )
```

profile of v0, /device:TPU:32, one launch (start us, length us, event | category | flops | bytes accessed | tf_op | source)
XLA Modules:
  0.0 53.0 jit_solution(13594274750644474025)
XLA Ops:
  0.0 22.7 %exchange.1 = (bf16[128,16,128]{2,1,0:T(8,128)(2,1)S(1)}, s32[128,128]{1,0:T(8,128)S(1)}, f32[64,128,128]{2,1,0:T(8,128)S(1)}, bf16[64,128,256]{2,1,0:T(8,128)(2...) custom-call(s32[1,128]{1,0:T(1,128)} %counts_ref.1, ...), custom_call_target="tpu_custom_call" | custom-call | tf_op jit(solution)/shard_map/exchange/pallas_call | solution.py:210
  22.7 5.1 %scatter.1 = (f32[9152,128]{1,0:T(8,128)S(1)}, f32[9152,128]{1,0:T(8,128)S(1)}, f32[9152,128]{1,0:T(8,128)S(1)}, f32[9152,128]{1,0:T(8,128)S(1)}, f32[136,128]{1...) custom-call(bf16[128,16,128]{2,1,0:T(8,128)(2,1)S(1)} %get-tuple-ele, ...), custom_call_target="tpu_custom_call", output_to_operand_aliasing={{0}: (2, {}), {1}: (3, {}), {2}: (4, {}), {3}: (5, {})} | custom-call | tf_op jit(solution)/shard_map/scatter/pallas_call | solution.py:330
  27.8 23.1 %steps.1.stage = f32[9216,128]{1,0:T(8,128)S(1)} custom-call(f32[9152,128]{1,0:T(8,128)S(1)} %get-tuple-element.31.acc0, f32[9152,128]{1,0:T(8,128)S(1)} %get-tuple-element.32.acc1, f32[9152,128]{1,0:T(8,128)S(1)} %get-tuple-element.33.acc2, f32[9152,128]{1,0:T(8,128)S(1)} %get-tuple-element.34.acc3, f32[136,128]{1,0:T(8,128)S(1)} %get-tuple-element.35.edge_e, ...), custom_call_target="tpu_custom_call" | custom-call | tf_op jit(solution)/shard_map/steps/pallas_call | solution.py:648
  50.9 2.1 %finish.1 = f32[128,64,128]{2,1,0:T(8,128)} custom-call(f32[9216,128]{1,0:T(8,128)S(1)} %steps.1.stage), custom_call_target="tpu_custom_call" | custom-call | tf_op jit(solution)/shard_map/finish/pallas_call | solution.py:692
where the time goes:
time: 53.1 us; the launch traced here: 53 us
  Pallas kernels  52.9 us (100%)
    pallas_call x1, Pallas kernels, steps(): pl.pallas_call(functools.partial(steps_body, n_gx, n_gy), out_shape=make(...  23.1 us
    pallas_call x1, Pallas kernels, exchange(): pl.pallas_call(functools.partial(exchange_body, n_gx, n_gy, unused_lat),...  22.7 us
    pallas_call x1, Pallas kernels, scatter(): pl.pallas_call(functools.partial(scatter_body, nx, ny), out_shape=(*[vm(a...  5.08 us
    pallas_call x1, Pallas kernels, finish(): pl.pallas_call(functools.partial(finish_body, parts), out_shape=jax.Shape...  2.07 us

commit v1 on v0

--- a/solution.py
+++ b/solution.py
@@ -46,21 +46,21 @@
     for copy in small + large:
         copy.start()
 
-    def peer(i):
-        y = lax.rem(lax.rem(gy, 4) + lax.rem(i, 4) + 2, 4)
-        z = lax.rem(lax.div(gy, 4) + lax.rem(lax.div(i, 4), 4) + n_gy // 8, n_gy // 4)
-        x = lax.rem(lax.div(gx, 2) + lax.rem(lax.div(i, n_gy), n_gx // 2) + n_gx // 4, n_gx // 2)
-        c = lax.rem(gx + lax.div(i, n_gy * (n_gx // 2)), 2)
-        return x * 2 + c, z * 4 + y
-
-    own = 2 + (n_gy // 8) * 4 + (n_gx // 4) * n_gy
+    turn = (2, 1, 3, 0)
+    depth = n_gy // 4
+    near = [lax.rem(lax.rem(gy, 4) + dy, 4) for dy in range(4)]
+    far = [lax.rem(lax.div(gy, 4) + dz, depth) * 4 for dz in range(depth)]
+    lines = [far[dz] + near[dy] for dz in turn[:depth] for dy in turn if (dz, dy) != (0, 0)]
 
     def each_peer(do):
-        for first, last in ((0, own), (own + 1, peers)):
-
-            @pl.loop(first, last)
-            def _(i):
-                do(*peer(i))
+        @pl.loop(0, n_gx)
+        def _(k):
+            x = lax.rem(gx + n_gx // 2 + k, n_gx)
+            for y in lines:
+                do(x, y)
+
+        for dx in range(1, n_gx):
+            do(lax.rem(gx + dx, n_gx), gy)
 
     barrier = pltpu.get_barrier_semaphore()
     each_peer(lambda x, y: pl.semaphore_signal(barrier, inc=1, device_id=(x, y), device_id_type=MESH))

time: 53.1 us -> 50.5 us (0.951)
  Pallas kernels: 52.9 us -> 50.4 us
    pallas_call x1, Pallas kernels: 22.7 us -> 19.7 us  [exchange(): pl.pallas_call(functools.partial(exchange_body, n_gx, n_gy, unused_lat),...]
where the time goes in v1:
time: 50.5 us; the launch traced here: 50.4 us
  Pallas kernels  50.4 us (100%)
    pallas_call x1, Pallas kernels, steps(): pl.pallas_call(functools.partial(steps_body, n_gx, n_gy), out_shape=make(...  23.5 us
    pallas_call x1, Pallas kernels, exchange(): pl.pallas_call(functools.partial(exchange_body, n_gx, n_gy, unused_lat),...  19.7 us
    pallas_call x1, Pallas kernels, scatter(): pl.pallas_call(functools.partial(scatter_body, nx, ny), out_shape=(*[vm(a...  5.08 us
    pallas_call x1, Pallas kernels, finish(): pl.pallas_call(functools.partial(finish_body, parts), out_shape=jax.Shape...  2.07 us

profile of v1, /device:TPU:32, one launch (start us, length us, event | category | flops | bytes accessed | tf_op | source)
XLA Modules:
  0.0 50.4 jit_solution(10753089548095981793)
XLA Ops:
  0.0 19.7 %exchange.1 = (bf16[128,16,128]{2,1,0:T(8,128)(2,1)S(1)}, s32[128,128]{1,0:T(8,128)S(1)}, f32[64,128,128]{2,1,0:T(8,128)S(1)}, bf16[64,128,256]{2,1,0:T(8,128)(2...) custom-call(s32[1,128]{1,0:T(1,128)} %counts_ref.1, ...), custom_call_target="tpu_custom_call" | custom-call | tf_op jit(solution)/shard_map/exchange/pallas_call | solution.py:210
  19.7 5.1 %scatter.1 = (f32[9152,128]{1,0:T(8,128)S(1)}, f32[9152,128]{1,0:T(8,128)S(1)}, f32[9152,128]{1,0:T(8,128)S(1)}, f32[9152,128]{1,0:T(8,128)S(1)}, f32[136,128]{1...) custom-call(bf16[128,16,128]{2,1,0:T(8,128)(2,1)S(1)} %get-tuple-ele, ...), custom_call_target="tpu_custom_call", output_to_operand_aliasing={{0}: (2, {}), {1}: (3, {}), {2}: (4, {}), {3}: (5, {})} | custom-call | tf_op jit(solution)/shard_map/scatter/pallas_call | solution.py:330
  24.8 23.5 %steps.1.stage = f32[9216,128]{1,0:T(8,128)S(1)} custom-call(f32[9152,128]{1,0:T(8,128)S(1)} %get-tuple-element.31.acc0, f32[9152,128]{1,0:T(8,128)S(1)} %get-tuple-element.32.acc1, f32[9152,128]{1,0:T(8,128)S(1)} %get-tuple-element.33.acc2, f32[9152,128]{1,0:T(8,128)S(1)} %get-tuple-element.34.acc3, f32[136,128]{1,0:T(8,128)S(1)} %get-tuple-element.35.edge_e, ...), custom_call_target="tpu_custom_call" | custom-call | tf_op jit(solution)/shard_map/steps/pallas_call | solution.py:648
  48.4 2.1 %finish.1 = f32[128,64,128]{2,1,0:T(8,128)} custom-call(f32[9216,128]{1,0:T(8,128)S(1)} %steps.1.stage), custom_call_target="tpu_custom_call" | custom-call | tf_op jit(solution)/shard_map/finish/pallas_call | solution.py:692

commit v2 on v1

--- a/solution.py
+++ b/solution.py
@@ -43,7 +43,7 @@
         pltpu.make_async_copy(inv_ref, inv_stage, load_sem.at[6]),
         pltpu.make_async_copy(state_ref, state_stage.reshape(nx, pitch, levels).at[:, 0:ny, :], load_sem.at[7]),
     ]
-    for copy in small + large:
+    for copy in small:
         copy.start()
 
     turn = (2, 1, 3, 0)
@@ -67,6 +67,8 @@
 
     for copy in small:
         copy.wait()
+    for copy in large:
+        copy.start()
     blocks = held // 128
     wide[0:held, :] = prof[...].astype(jnp.float32)
     wide[held:held + CAP, :] = jnp.zeros((CAP, levels), jnp.float32)
@@ -119,19 +121,19 @@
             halo(3, high_stage.at[1], inv_halo.at[1], gx, up)]
     to_s = [halo(4, row_stage.at[0], diff_rows.at[0], gx, down),
             halo(5, high_stage.at[0], inv_halo.at[0], gx, down)]
+    pl.semaphore_wait(barrier, peers - 1)
+
+    def send(x, y):
+        to = x * n_gy + y
+        remote(prof_send.at[to], prof_out.at[me], psend, precv, x, y).start()
+        remote(meta_send.at[pl.ds(to, 1)], meta_out.at[pl.ds(me, 1)], msend, mrecv, x, y).start()
+
+    each_peer(send)
     large[0].wait()
     large[1].wait()
     for k, y in ((0, 0), (1, ny - 1)):
         row_stage[k] = diff_stage[pl.ds(y, nx, stride=pitch), :].astype(jnp.bfloat16)
         high_stage[k] = inv_stage[y].astype(jnp.bfloat16)
-    pl.semaphore_wait(barrier, peers - 1)
-
-    def send(x, y):
-        to = x * n_gy + y
-        remote(prof_send.at[to], prof_out.at[me], psend, precv, x, y).start()
-        remote(meta_send.at[pl.ds(to, 1)], meta_out.at[pl.ds(me, 1)], msend, mrecv, x, y).start()
-
-    each_peer(send)
     to_e.start()
     to_w.start()
 

time: 50.5 us -> 50.5 us (level)
  no operation moved by 1% of the time
where the time goes in v2:
time: 50.5 us; the launch traced here: 50.4 us
  Pallas kernels  50.4 us (100%)
    pallas_call x1, Pallas kernels, steps(): pl.pallas_call(functools.partial(steps_body, n_gx, n_gy), out_shape=make(...  23.5 us
    pallas_call x1, Pallas kernels, exchange(): pl.pallas_call(functools.partial(exchange_body, n_gx, n_gy, unused_lat),...  19.7 us
    pallas_call x1, Pallas kernels, scatter(): pl.pallas_call(functools.partial(scatter_body, nx, ny), out_shape=(*[vm(a...  5.07 us
    pallas_call x1, Pallas kernels, finish(): pl.pallas_call(functools.partial(finish_body, parts), out_shape=jax.Shape...  2.07 us

profile of v2, /device:TPU:32, one launch (start us, length us, event | category | flops | bytes accessed | tf_op | source)
XLA Modules:
  0.0 50.4 jit_solution(10782017330919063642)
XLA Ops:
  0.0 19.7 %exchange.1 = (bf16[128,16,128]{2,1,0:T(8,128)(2,1)S(1)}, s32[128,128]{1,0:T(8,128)S(1)}, f32[64,128,128]{2,1,0:T(8,128)S(1)}, bf16[64,128,256]{2,1,0:T(8,128)(2...) custom-call(s32[1,128]{1,0:T(1,128)} %counts_ref.1, ...), custom_call_target="tpu_custom_call" | custom-call | tf_op jit(solution)/shard_map/exchange/pallas_call | solution.py:212
  19.7 5.1 %scatter.1 = (f32[9152,128]{1,0:T(8,128)S(1)}, f32[9152,128]{1,0:T(8,128)S(1)}, f32[9152,128]{1,0:T(8,128)S(1)}, f32[9152,128]{1,0:T(8,128)S(1)}, f32[136,128]{1...) custom-call(bf16[128,16,128]{2,1,0:T(8,128)(2,1)S(1)} %get-tuple-ele, ...), custom_call_target="tpu_custom_call", output_to_operand_aliasing={{0}: (2, {}), {1}: (3, {}), {2}: (4, {}), {3}: (5, {})} | custom-call | tf_op jit(solution)/shard_map/scatter/pallas_call | solution.py:332
  24.8 23.5 %steps.1.stage = f32[9216,128]{1,0:T(8,128)S(1)} custom-call(f32[9152,128]{1,0:T(8,128)S(1)} %get-tuple-element.31.acc0, f32[9152,128]{1,0:T(8,128)S(1)} %get-tuple-element.32.acc1, f32[9152,128]{1,0:T(8,128)S(1)} %get-tuple-element.33.acc2, f32[9152,128]{1,0:T(8,128)S(1)} %get-tuple-element.34.acc3, f32[136,128]{1,0:T(8,128)S(1)} %get-tuple-element.35.edge_e, ...), custom_call_target="tpu_custom_call" | custom-call | tf_op jit(solution)/shard_map/steps/pallas_call | solution.py:650
  48.3 2.1 %finish.1 = f32[128,64,128]{2,1,0:T(8,128)} custom-call(f32[9216,128]{1,0:T(8,128)S(1)} %steps.1.stage), custom_call_target="tpu_custom_call" | custom-call | tf_op jit(solution)/shard_map/finish/pallas_call | solution.py:694

commit v3 on v2

--- a/solution.py
+++ b/solution.py
@@ -354,7 +354,7 @@
 
 
 STEPS = 4
-CHUNK = 16
+CHUNK = 8
 
 
 def steps_body(n_gx, n_gy, acc0, acc1, acc2, acc3, edge_e, edge_w, edge_n, edge_s, knot,

time: 50.5 us -> 51 us (level)
    pallas_call x1, Pallas kernels: 23.5 us -> 24.1 us  [steps(): pl.pallas_call(functools.partial(steps_body, n_gx, n_gy), out_shape=make(...]
where the time goes in v3:
time: 51 us; the launch traced here: 50.9 us
  Pallas kernels  50.9 us (100%)
    pallas_call x1, Pallas kernels, steps(): pl.pallas_call(functools.partial(steps_body, n_gx, n_gy), out_shape=make(...  24.1 us
    pallas_call x1, Pallas kernels, exchange(): pl.pallas_call(functools.partial(exchange_body, n_gx, n_gy, unused_lat),...  19.7 us
    pallas_call x1, Pallas kernels, scatter(): pl.pallas_call(functools.partial(scatter_body, nx, ny), out_shape=(*[vm(a...  5.07 us
    pallas_call x1, Pallas kernels, finish(): pl.pallas_call(functools.partial(finish_body, parts), out_shape=jax.Shape...  2.07 us

profile of v3, /device:TPU:32, one launch (start us, length us, event | category | flops | bytes accessed | tf_op | source)
XLA Modules:
  0.0 50.9 jit_solution(13506595275858149583)
XLA Ops:
  0.0 19.7 %exchange.1 = (bf16[128,16,128]{2,1,0:T(8,128)(2,1)S(1)}, s32[128,128]{1,0:T(8,128)S(1)}, f32[64,128,128]{2,1,0:T(8,128)S(1)}, bf16[64,128,256]{2,1,0:T(8,128)(2...) custom-call(s32[1,128]{1,0:T(1,128)} %counts_ref.1, ...), custom_call_target="tpu_custom_call" | custom-call | tf_op jit(solution)/shard_map/exchange/pallas_call | solution.py:212
  19.7 5.1 %scatter.1 = (f32[9152,128]{1,0:T(8,128)S(1)}, f32[9152,128]{1,0:T(8,128)S(1)}, f32[9152,128]{1,0:T(8,128)S(1)}, f32[9152,128]{1,0:T(8,128)S(1)}, f32[136,128]{1...) custom-call(bf16[128,16,128]{2,1,0:T(8,128)(2,1)S(1)} %get-tuple-ele, ...), custom_call_target="tpu_custom_call", output_to_operand_aliasing={{0}: (2, {}), {1}: (3, {}), {2}: (4, {}), {3}: (5, {})} | custom-call | tf_op jit(solution)/shard_map/scatter/pallas_call | solution.py:332
  24.8 24.1 %steps.1.stage = f32[9216,128]{1,0:T(8,128)S(1)} custom-call(f32[9152,128]{1,0:T(8,128)S(1)} %get-tuple-element.31.acc0, f32[9152,128]{1,0:T(8,128)S(1)} %get-tuple-element.32.acc1, f32[9152,128]{1,0:T(8,128)S(1)} %get-tuple-element.33.acc2, f32[9152,128]{1,0:T(8,128)S(1)} %get-tuple-element.34.acc3, f32[136,128]{1,0:T(8,128)S(1)} %get-tuple-element.35.edge_e, ...), custom_call_target="tpu_custom_call" | custom-call | tf_op jit(solution)/shard_map/steps/pallas_call | solution.py:650
  48.9 2.1 %finish.1 = f32[128,64,128]{2,1,0:T(8,128)} custom-call(f32[9216,128]{1,0:T(8,128)S(1)} %steps.1.stage), custom_call_target="tpu_custom_call" | custom-call | tf_op jit(solution)/shard_map/finish/pallas_call | solution.py:694
